TPU v7x, 32 devices: a whole 2x2x4 slice. The times are simulated.
32 devices in a mesh: lat: 8 (over z, y), rad: 4 (over x, core).
Axes of the slice: x: 2, y: 2, z: 4, core: 2. Of those that a mesh axis runs over, the one named last changes fastest.
Arguments:
- displacement: float32 [64, 6144], P('rad', 'lat'), may hold values from -6 to 6
- surface_load: float32 [64, 6144], P('rad', 'lat'), may hold values from -6 to 6
- dens_grad: float32 [64, 6144], P('rad', 'lat'), may hold values from 0.5 to 2
- dens_ref: float32 [64], P('rad'), may hold values from 0.5 to 2
- relax_rate: float32 [64, 6144], P('rad', 'lat'), may hold values from 0.02 to 0.2
- basis: bfloat16 [2408, 6144], P(None, 'lat'), may hold values from -0.109375 to 0.109375
- neighbours: int32 [4, 6144], P(None, 'lat'), may hold values from 0 to 767
- green: float32 [49, 64, 64], replicated, may hold values from -2.5 to 2.5
Outputs:
- relaxed: float32 [64, 6144], P('rad', 'lat')
- step_sizes: float32 [3], replicated
Inputs may be any that keep to these rules, and one draw needn't show every extreme that they name: `neighbours`: indices of columns inside the same tile of 768 columns.
All inputs are finite; a program needn't handle non-finite values.
Results may differ from a plain program's by a relative error of at most 0.0045.
Values may be sent and summed in bfloat16 or wider, within the bound.
No kernel may reach another device: no remote copies, remote signals or barrier semaphores. Data moves between devices by JAX's collectives and lax.ppermute only.
A program may use at most 64 MiB of HBM per device.

v0:
```python
import jax
import jax.numpy as jnp
from jax import lax
from jax.sharding import PartitionSpec as P

DEG = 48
L = 64
ITERS = 3
KH = 2401


def extended(shard, sides, width):
    for axis, dim in sides:
        size, length = (lax.axis_size(axis), shard.shape[dim])
        up = [(i, (i + 1) % size) for i in range(size - 1)]
        down = [(j, i) for i, j in up]
        last = lax.slice_in_dim(shard, length - width, length, axis=dim)
        first = lax.slice_in_dim(shard, 0, width, axis=dim)
        before = lax.ppermute(last, axis, up)
        after = lax.ppermute(first, axis, down)
        shard = jnp.concatenate([before, shard, after], axis=dim)
    return shard


def apply_degrees(coefs, green_rows):
    blocks = []
    for degree in range(DEG + 1):
        rows = coefs[degree * degree : (degree + 1) * (degree + 1)]
        blocks.append(
            lax.dot_general(
                rows,
                green_rows[degree],
                (((1,), (1,)), ((), ())),
                precision=lax.Precision.HIGHEST,
                preferred_element_type=jnp.float32,
            )
        )
    blocks.append(jnp.zeros((coefs.shape[0] - KH, green_rows.shape[1]), jnp.float32))
    return jnp.concatenate(blocks, axis=0).astype(jnp.bfloat16)


def local(displacement, surface_load, dens_grad, dens_ref, relax_rate, basis, neighbours, green):
    u = displacement
    layers, columns = u.shape
    lat_count = lax.axis_size("lat")
    green_rows = lax.dynamic_slice_in_dim(green, lax.axis_index("rad") * layers, layers, 1)
    sizes = []
    for it in range(ITERS):
        padded = extended(u, (("rad", 0),), 1)
        rho = (dens_grad * u + dens_ref[:, None] * (padded[2:] - padded[:-2]) * 0.5).astype(
            jnp.bfloat16
        )
        partial_sums = lax.dot_general(
            basis, rho, (((1,), (1,)), ((), ())), preferred_element_type=jnp.float32
        )
        summed = lax.psum(partial_sums, "lat")
        coefs = lax.all_gather(summed, "rad", axis=1, tiled=True)
        phi = apply_degrees(coefs, green_rows)
        potential = lax.dot_general(
            phi, basis, (((0,), (0,)), ((), ())), preferred_element_type=jnp.float32
        )
        outer = extended(potential, (("rad", 0),), 1)
        force = (outer[2:] - outer[:-2]) * 0.5
        lap = jnp.sum(u[:, neighbours], axis=1) - 4.0 * u
        new = u + relax_rate * (surface_load + force + lap - u)
        squared = jnp.sum((new - u) ** 2)
        sizes.append(squared)
        u = new
    totals = jnp.stack(sizes)
    totals = lax.psum(totals, ("lat", "rad"))
    return (u, jnp.sqrt(totals / (L * columns * lat_count)))


def solution(mesh):
    placed = (
        P("rad", "lat"),
        P("rad", "lat"),
        P("rad", "lat"),
        P("rad"),
        P("rad", "lat"),
        P(None, "lat"),
        P(None, "lat"),
        P(),
    )
    return jax.shard_map(
        local, mesh=mesh, in_specs=placed, out_specs=(P("rad", "lat"), P()), check_vma=False
    )
```

profile of v0, /device:TPU:0, one launch (start us, length us, event | category | flops | bytes accessed | tf_op | source)
XLA Modules:
  0.0 424.7 jit_solution(13441633414190941219)
XLA Ops:
  8.1 2.4 collective-permute-start.1
  11.8 3.8 collective-permute-done
  15.6 3.9 convolution_bitcast_fusion.2
  19.7 72.3 %all-reduce.4.cloned.1.call-done = f32[2408,16]{0,1:T(8,128)} async-done(((f32[2408,16]{0,1:T(8,128)}), f32[2408,16]{0,1:T(8,128)}) %all-reduce.4.cloned.1.call-update) | async-done | bytes 154128 | tf_op jit(solution)/shard_map/psum | solution.py:56
  92.0 7.9 %all_gather.9 = f32[2408,64]{0,1:T(8,128)S(1)} all-gather(f32[2408,16]{0,1:T(8,128)} %all-reduce.4.cloned.1.call-done), channel_id=1, replica_groups=mesh['lat'=8,'rad'=4] {'rad'}, dimensions={1}, use_global_device_ids=true | all-gather | bytes 770560 | tf_op jit(solution)/shard_map/all_gather | solution.py:57
  112.0 2.7 fusion.407
  118.4 10.8 %gather_fusion = f32[3072,16]{1,0:T(8,128)} fusion(f32[16,768]{0,1:T(8,128)S(1)} %copy.24, s32[3072]{0:T(1024)S(1)} %broadcast_clamp_fusion), kind=kCustom, calls=%fused_computation | custom fusion | bytes 405504 | tf_op jit(solution)/shard_map/gather | solution.py:64
  131.1 3.0 collective-permute-start.5
  135.5 2.8 collective-permute-done.4
  138.3 3.8 convolution_bitcast_fusion.1
  142.1 70.9 %all-reduce.6.cloned.1.call-done = f32[2408,16]{0,1:T(8,128)} async-done(((f32[2408,16]{0,1:T(8,128)}), f32[2408,16]{0,1:T(8,128)}) %all-reduce.6.cloned.1.call-update) | async-done | bytes 154128 | tf_op jit(solution)/shard_map/psum | solution.py:56
  213.1 7.9 %all_gather.10 = f32[2408,64]{0,1:T(8,128)S(1)} all-gather(f32[2408,16]{0,1:T(8,128)} %all-reduce.6.cloned.1.call-done), channel_id=1, replica_groups=mesh['lat'=8,'rad'=4] {'rad'}, dimensions={1}, use_global_device_ids=true | all-gather | bytes 770560 | tf_op jit(solution)/shard_map/all_gather | solution.py:57
  233.1 2.6 fusion.408
  235.7 2.3 collective-permute-start.7
  239.4 10.8 %gather_fusion.1 = f32[3072,16]{1,0:T(8,128)} fusion(f32[16,768]{0,1:T(8,128)S(1)} %copy.34, s32[3072]{0:T(1024)S(1)} %broadcast_clamp_fusion), kind=kCustom, calls=%fused_computation.1 | custom fusion | bytes 405504 | tf_op jit(solution)/shard_map/gather | solution.py:64
  252.0 3.0 collective-permute-start.9
  256.4 2.8 collective-permute-done.8
  259.2 3.8 convolution_bitcast_fusion
  263.0 71.0 %all-reduce.8.cloned.1.call-done = f32[2408,16]{0,1:T(8,128)} async-done(((f32[2408,16]{0,1:T(8,128)}), f32[2408,16]{0,1:T(8,128)}) %all-reduce.8.cloned.1.call-update) | async-done | bytes 154128 | tf_op jit(solution)/shard_map/psum | solution.py:56
  334.0 8.1 %all_gather.11 = f32[2408,64]{0,1:T(8,128)S(1)} all-gather(f32[2408,16]{0,1:T(8,128)} %all-reduce.8.cloned.1.call-done), channel_id=1, replica_groups=mesh['lat'=8,'rad'=4] {'rad'}, dimensions={1}, use_global_device_ids=true | all-gather | bytes 770560 | tf_op jit(solution)/shard_map/all_gather | solution.py:57
  354.2 2.6 fusion.409
  356.8 2.3 collective-permute-start.11
  360.6 10.8 %gather_fusion.2 = f32[3072,16]{1,0:T(8,128)} fusion(f32[16,768]{0,1:T(8,128)S(1)} %copy.44, s32[3072]{0:T(1024)S(1)} %broadcast_clamp_fusion), kind=kCustom, calls=%fused_computation.2 | custom fusion | bytes 405504 | tf_op jit(solution)/shard_map/gather | solution.py:64
  376.4 41.3 %psum.31 = f32[3]{0:T(128)S(1)} all-reduce(f32[3]{0:T(128)S(1)} %pad_maximum_fusion.12), channel_id=1, replica_groups=mesh['lat'=8,'rad'=4] {'lat','rad'}, use_global_device_ids=true, to_apply=%region_9.0 | all-reduce | flops 3 | bytes 24 | tf_op jit(solution)/shard_map/psum | solution.py:70
  (237 shorter events, 56.8 us)
Async XLA Ops:
  7.2 92.8 %copy-start = (f32[49,64,64]{2,1,0:T(8,128)S(1)}, f32[49,64,64]{2,1,0:T(8,128)}, u32[]{:S(2)}) copy-start(f32[49,64,64]{2,1,0:T(8,128)} %param.15) | copy-start | bytes 2408452
  7.2 84.8 %all-reduce.4.cloned.1.call-start = ((), (), s32[]{:S(2)}) async-start(), calls=%async_computation | async-start | bytes 311296 | tf_op jit(solution)/shard_map/psum | solution.py:56
  8.1 3.7 collective-permute-start.1
  10.5 5.2 %collective-permute-start = (f32[1,768]{1,0:T(1,128)S(1)}, f32[1,768]{1,0:T(1,128)S(1)}, u32[]{:S(2)}, u32[]{:S(2)}) collective-permute-start(f32[1,768]{1,0:T(1,128)S(1)} %get-tuple-element.16), channel_id=1, source_target_pairs={{1,0},{2,1},{3,2},{5,4},{6,5},{7,6},{9,8},{10,9},{11,10},{13,12},{... | collective-permute-start | bytes 9224 | tf_op jit(solution)/shard_map/ppermute | solution.py:20
  11.8 7.8 %copy-start.5 = (s32[4,768]{1,0:T(4,128)S(1)}, s32[4,768]{1,0:T(4,128)}, u32[]{:S(2)}) copy-start(s32[4,768]{1,0:T(4,128)} %param.14) | copy-start | bytes 36868
  19.6 193.5 %all-reduce.6.cloned.1.call-start = ((), (), s32[]{:S(2)}) async-start(), calls=%async_computation.1 | async-start | bytes 311296 | tf_op jit(solution)/shard_map/psum | solution.py:56
  112.0 6.3 %copy-start.1 = (f32[16,768]{1,0:T(8,128)S(1)}, f32[16,768]{1,0:T(8,128)}, u32[]{:S(2)}) copy-start(f32[16,768]{1,0:T(8,128)} %param.8) | copy-start | bytes 147460
  114.7 16.3 %collective-permute-start.3 = (f32[1,768]{1,0:T(1,128)S(1)}, f32[1,768]{1,0:T(1,128)S(1)}, u32[]{:S(2)}, u32[]{:S(2)}) collective-permute-start(f32[1,768]{1,0:T(1,128)S(1)} %get-tuple-element.15), channel_id=1, source_target_pairs={{0,1},{1,2},{2,3},{4,5},{5,6},{6,7},{8,9},{9,10},{10,11},{12,13},{... | collective-permute-start | bytes 9224 | tf_op jit(solution)/shard_map/ppermute | solution.py:19
  116.9 14.1 %collective-permute-start.2 = (f32[1,768]{1,0:T(1,128)S(1)}, f32[1,768]{1,0:T(1,128)S(1)}, u32[]{:S(2)}, u32[]{:S(2)}) collective-permute-start(f32[1,768]{1,0:T(1,128)S(1)} %get-tuple-element.14), channel_id=1, source_target_pairs={{1,0},{2,1},{3,2},{5,4},{6,5},{7,6},{9,8},{10,9},{11,10},{13,12},{... | collective-permute-start | bytes 9224 | tf_op jit(solution)/shard_map/ppermute | solution.py:20
  129.3 1.8 copy-start.3
  129.3 1.8 copy-start.4
  129.3 9.0 %copy-start.2 = (f32[16,768]{1,0:T(8,128)S(1)}, f32[16,768]{1,0:T(8,128)}, u32[]{:S(2)}) copy-start(f32[16,768]{1,0:T(8,128)} %param.10) | copy-start | bytes 147460
  129.3 9.0 %copy-start.6 = (f32[16]{0:T(128)S(1)}, f32[16]{0:T(128)}, u32[]{:S(2)}) copy-start(f32[16]{0:T(128)} %param.11) | copy-start | bytes 196
  131.1 4.3 %collective-permute-start.5 = (f32[1,768]{1,0:T(1,128)S(1)}, f32[1,768]{1,0:T(1,128)S(1)}, u32[]{:S(2)}, u32[]{:S(2)}) collective-permute-start(f32[1,768]{1,0:T(1,128)S(1)} %get-tuple-element.13), channel_id=1, source_target_pairs={{0,1},{1,2},{2,3},{4,5},{5,6},{6,7},{8,9},{9,10},{10,11},{12,13},{... | collective-permute-start | bytes 9224 | tf_op jit(solution)/shard_map/ppermute | solution.py:19
  134.1 4.1 collective-permute-start.4
  142.1 191.9 %all-reduce.8.cloned.1.call-start = ((), (), s32[]{:S(2)}) async-start(), calls=%async_computation.2 | async-start | bytes 311296 | tf_op jit(solution)/shard_map/psum | solution.py:56
  235.7 16.2 %collective-permute-start.7 = (f32[1,768]{1,0:T(1,128)S(1)}, f32[1,768]{1,0:T(1,128)S(1)}, u32[]{:S(2)}, u32[]{:S(2)}) collective-permute-start(f32[1,768]{1,0:T(1,128)S(1)} %get-tuple-element.11), channel_id=1, source_target_pairs={{0,1},{1,2},{2,3},{4,5},{5,6},{6,7},{8,9},{9,10},{10,11},{12,13},{... | collective-permute-start | bytes 9224 | tf_op jit(solution)/shard_map/ppermute | solution.py:19
  238.0 14.0 %collective-permute-start.6 = (f32[1,768]{1,0:T(1,128)S(1)}, f32[1,768]{1,0:T(1,128)S(1)}, u32[]{:S(2)}, u32[]{:S(2)}) collective-permute-start(f32[1,768]{1,0:T(1,128)S(1)} %get-tuple-element.10), channel_id=1, source_target_pairs={{1,0},{2,1},{3,2},{5,4},{6,5},{7,6},{9,8},{10,9},{11,10},{13,12},{... | collective-permute-start | bytes 9224 | tf_op jit(solution)/shard_map/ppermute | solution.py:20
  252.0 4.3 %collective-permute-start.9 = (f32[1,768]{1,0:T(1,128)S(1)}, f32[1,768]{1,0:T(1,128)S(1)}, u32[]{:S(2)}, u32[]{:S(2)}) collective-permute-start(f32[1,768]{1,0:T(1,128)S(1)} %get-tuple-element.9), channel_id=1, source_target_pairs={{0,1},{1,2},{2,3},{4,5},{5,6},{6,7},{8,9},{9,10},{10,11},{12,13},{... | collective-permute-start | bytes 9224 | tf_op jit(solution)/shard_map/ppermute | solution.py:19
  255.1 4.1 collective-permute-start.8
  356.8 16.2 %collective-permute-start.11 = (f32[1,768]{1,0:T(1,128)S(1)}, f32[1,768]{1,0:T(1,128)S(1)}, u32[]{:S(2)}, u32[]{:S(2)}) collective-permute-start(f32[1,768]{1,0:T(1,128)S(1)} %get-tuple-element.7), channel_id=1, source_target_pairs={{0,1},{1,2},{2,3},{4,5},{5,6},{6,7},{8,9},{9,10},{10,11},{12,13},{... | collective-permute-start | bytes 9224 | tf_op jit(solution)/shard_map/ppermute | solution.py:19
  359.1 14.0 %collective-permute-start.10 = (f32[1,768]{1,0:T(1,128)S(1)}, f32[1,768]{1,0:T(1,128)S(1)}, u32[]{:S(2)}, u32[]{:S(2)}) collective-permute-start(f32[1,768]{1,0:T(1,128)S(1)} %get-tuple-element.6), channel_id=1, source_target_pairs={{1,0},{2,1},{3,2},{5,4},{6,5},{7,6},{9,8},{10,9},{11,10},{13,12},{... | collective-permute-start | bytes 9224 | tf_op jit(solution)/shard_map/ppermute | solution.py:20
Sparse Core Ops, SparseCore 0:
  19.7 72.2 all-reduce.3
  142.2 70.8 all-reduce.5
  263.1 70.8 all-reduce.7
where the time goes:
time: 426 us; the launch traced here: 425 us
  waiting for transfers between devices  224 us (53%)
  blocking collectives  65.1 us (15%)
  matrix products  52.3 us (12%)
  local copies, waits for them, and re-layouts  37.5 us (9%)
  starting transfers between devices  23.1 us (5%)
  between operations  14.2 us (3%)
  other arithmetic  8.64 us (2%)
    psum x3, waiting for transfers between devices, local(): summed = lax.psum(partial_sums, 'lat')  214 us
    psum x1, blocking collectives, local(): totals = lax.psum(totals, ('lat', 'rad'))  41.3 us
    dot_general x147, matrix products, apply_degrees(): lax.dot_general(rows, green_rows[degree], (((1,), (1,)), ((), ())), preci...  32.9 us
    gather x3, local copies, waits for them, and re-layouts, local(): lap = jnp.sum(u[:, neighbours], axis=1) - 4.0 * u  32.5 us
    all_gather x3, blocking collectives, local(): coefs = lax.all_gather(summed, 'rad', axis=1, tiled=True)  23.9 us
    ppermute x6, starting transfers between devices, extended(): before = lax.ppermute(last, axis, up)  15.2 us
    dot_general x3, matrix products, local(): lax.dot_general(basis, rho, (((1,), (1,)), ((), ())), preferred_element_t...  11.5 us
    ppermute x6, waiting for transfers between devices, extended(): after = lax.ppermute(first, axis, down)  9.47 us
  transfers between devices with their start and end apart: 15, of which 6 were waited for; matrix products, arithmetic and copies ran while one was open for 9% of the time, Pallas kernels for 0%

commit v1 on v0

--- a/solution.py
+++ b/solution.py
@@ -7,6 +7,17 @@
 L = 64
 ITERS = 3
 KH = 2401
+
+
+def finish_edges_all(axis_tag, x_in):
+    workers = jax.lax.axis_size(axis_tag)
+    x_new = x_in
+    for j0 in [tick for tick in (1, 2, 4, 8, 16) if tick < workers]:
+        entries = []
+        for dd in [*range(workers)]:
+            entries.append((dd, dd ^ j0))
+        x_new = x_new + jax.lax.ppermute(x_new, axis_tag, entries)
+    return x_new
 
 
 def extended(shard, sides, width):
@@ -53,7 +64,7 @@
         partial_sums = lax.dot_general(
             basis, rho, (((1,), (1,)), ((), ())), preferred_element_type=jnp.float32
         )
-        summed = lax.psum(partial_sums, "lat")
+        summed = finish_edges_all("lat", partial_sums)
         coefs = lax.all_gather(summed, "rad", axis=1, tiled=True)
         phi = apply_degrees(coefs, green_rows)
         potential = lax.dot_general(

time: 426 us -> 262 us (0.62)
  waiting for transfers between devices: 224 us -> 64.8 us
  starting transfers between devices: 23.1 us -> 37.3 us
  between operations: 14.2 us -> 1.1 us
    psum x3 -> x0, waiting for transfers between devices: 214 us -> none  [local(): summed = lax.psum(partial_sums, 'lat')]
    ppermute x0 -> x9, waiting for transfers between devices: none -> 55 us  [finish_edges_all(): x_new = x_new + jax.lax.ppermute(x_new, axis_tag, entries)]
    ppermute x0 -> x9, starting transfers between devices: none -> 12.8 us  [finish_edges_all(): x_new = x_new + jax.lax.ppermute(x_new, axis_tag, entries)]
  transfers between devices with their start and end apart: 15 -> 21, of which waited for: 6 -> 12; matrix products, arithmetic and copies ran while one was open for 9% -> 15% of each run, Pallas kernels for 0% -> 0%
where the time goes in v1:
time: 262 us; the launch traced here: 261 us
  waiting for transfers between devices  64.8 us (25%)
  blocking collectives  61 us (23%)
  matrix products  50.3 us (19%)
  local copies, waits for them, and re-layouts  37.6 us (14%)
  starting transfers between devices  37.3 us (14%)
  other arithmetic  8.83 us (3%)
    ppermute x9, waiting for transfers between devices, finish_edges_all(): x_new = x_new + jax.lax.ppermute(x_new, axis_tag, entries)  55 us
    psum x1, blocking collectives, local(): totals = lax.psum(totals, ('lat', 'rad'))  40 us
    dot_general x147, matrix products, apply_degrees(): lax.dot_general(rows, green_rows[degree], (((1,), (1,)), ((), ())), preci...  32.9 us
    gather x3, local copies, waits for them, and re-layouts, local(): lap = jnp.sum(u[:, neighbours], axis=1) - 4.0 * u  32.5 us
    all_gather x3, blocking collectives, local(): coefs = lax.all_gather(summed, 'rad', axis=1, tiled=True)  21 us
    ppermute x6, starting transfers between devices, extended(): before = lax.ppermute(last, axis, up)  16.7 us
    ppermute x9, starting transfers between devices, finish_edges_all(): x_new = x_new + jax.lax.ppermute(x_new, axis_tag, entries)  12.8 us
    ppermute x6, waiting for transfers between devices, extended(): after = lax.ppermute(first, axis, down)  9.83 us
  transfers between devices with their start and end apart: 21, of which 12 were waited for; matrix products, arithmetic and copies ran while one was open for 15% of the time, Pallas kernels for 0%

profile of v1, /device:TPU:0, one launch (start us, length us, event | category | flops | bytes accessed | tf_op | source)
XLA Modules:
  0.0 260.9 jit_solution(5909004982219384565)
XLA Ops:
  5.2 3.8 %collective-permute-done = f32[1,768]{1,0:T(1,128)S(1)} collective-permute-done((f32[1,768]{1,0:T(1,128)S(1)}, f32[1,768]{1,0:T(1,128)S(1)}, u32[]{:S(2)}, u32[]{:S(2)}) %collective-permute-start) | collective-permute-done | bytes 3104 | tf_op jit(solution)/shard_map/ppermute | solution.py:31
  9.1 3.2 %convolution_bitcast_fusion.2 = f32[2408,16]{0,1:T(8,128)S(1)} fusion(bf16[2408,768]{1,0:T(8,128)(2,1)} %param.13, f32[16,768]{1,0:T(8,128)} %param.8, f32[1,768]{1,0:T(1,128)S(1)} %collective-permute-done.1, f32[1,768]{1,0:T(1,128)S(1)} %collective-permute-done, f32[16,768]{1,0:T(8,128)} %param.10, f32[16]{0:T(128)} %param.11), kind=kOutput, calls=%fused_computation.5 | convolution fusion | flops 59277312 | bytes 3957312 | tf_op jit(solution)/shard_map/dot_general | solution.py:64
  13.9 4.0 %collective-permute-done.2 = f32[2408,16]{0,1:T(8,128)S(1)} collective-permute-done((f32[2408,16]{0,1:T(8,128)S(1)}, f32[2408,16]{0,1:T(8,128)S(1)}, u32[]{:S(2)}, u32[]{:S(2)}) %collective-permute-start.2) | collective-permute-done | bytes 154144 | tf_op jit(solution)/shard_map/ppermute | solution.py:19
  19.5 5.1 %collective-permute-done.3 = f32[2408,16]{0,1:T(8,128)S(1)} collective-permute-done((f32[2408,16]{0,1:T(8,128)S(1)}, f32[2408,16]{0,1:T(8,128)S(1)}, u32[]{:S(2)}, u32[]{:S(2)}) %collective-permute-start.3) | collective-permute-done | bytes 154144 | tf_op jit(solution)/shard_map/ppermute | solution.py:19
  27.3 7.7 %collective-permute-done.4 = f32[2408,16]{0,1:T(8,128)S(1)} collective-permute-done((f32[2408,16]{0,1:T(8,128)S(1)}, f32[2408,16]{0,1:T(8,128)S(1)}, u32[]{:S(2)}, u32[]{:S(2)}) %collective-permute-start.4) | collective-permute-done | bytes 154144 | tf_op jit(solution)/shard_map/ppermute | solution.py:19
  35.0 6.8 %all_gather.9 = f32[2408,64]{0,1:T(8,128)S(1)} all-gather(f32[2408,16]{0,1:T(8,128)S(1)} %add.76), channel_id=1, replica_groups=mesh['lat'=8,'rad'=4] {'rad'}, dimensions={1}, use_global_device_ids=true | all-gather | bytes 770560 | tf_op jit(solution)/shard_map/all_gather | solution.py:68
  60.3 10.8 %gather_fusion = f32[3072,16]{1,0:T(8,128)} fusion(f32[16,768]{0,1:T(8,128)S(1)} %copy.24, s32[3072]{0:T(1024)S(1)} %broadcast_clamp_fusion), kind=kCustom, calls=%fused_computation | custom fusion | bytes 405504 | tf_op jit(solution)/shard_map/gather | solution.py:75
  73.0 3.8 %collective-permute-start.8 = (f32[1,768]{1,0:T(1,128)S(1)}, f32[1,768]{1,0:T(1,128)S(1)}, u32[]{:S(2)}, u32[]{:S(2)}) collective-permute-start(f32[1,768]{1,0:T(1,128)S(1)} %get-tuple-element.13), channel_id=1, source_target_pairs={{0,1},{1,2},{2,3},{4,5},{5,6},{6,7},{8,9},{9,10},{10,11},{12,13},{... | collective-permute-start | bytes 9224 | tf_op jit(solution)/shard_map/ppermute | solution.py:30
  78.1 3.0 %collective-permute-done.7 = f32[1,768]{1,0:T(1,128)S(1)} collective-permute-done((f32[1,768]{1,0:T(1,128)S(1)}, f32[1,768]{1,0:T(1,128)S(1)}, u32[]{:S(2)}, u32[]{:S(2)}) %collective-permute-start.7) | collective-permute-done | bytes 3104 | tf_op jit(solution)/shard_map/ppermute | solution.py:31
  81.1 3.1 %convolution_bitcast_fusion.1 = f32[2408,16]{0,1:T(8,128)S(1)} fusion(bf16[2408,768]{1,0:T(8,128)(2,1)} %param.13, f32[16,768]{1,0:T(8,128)S(1)} %fusion.36, f32[1,768]{1,0:T(1,128)S(1)} %collective-permute-done.8, f32[1,768]{1,0:T(1,128)S(1)} %collective-permute-done.7, f32[16,768]{1,0:T(8,128)S(1)} %copy-done.2, f32[16]{0:T(128)S(1)} %copy-done.6), kind=kOutput, calls=%fused_computation.4 | convolution fusion | flops 59277312 | bytes 3957312 | tf_op jit(solution)/shard_map/dot_general | solution.py:64
  85.8 4.0 %collective-permute-done.9 = f32[2408,16]{0,1:T(8,128)S(1)} collective-permute-done((f32[2408,16]{0,1:T(8,128)S(1)}, f32[2408,16]{0,1:T(8,128)S(1)}, u32[]{:S(2)}, u32[]{:S(2)}) %collective-permute-start.9) | collective-permute-done | bytes 154144 | tf_op jit(solution)/shard_map/ppermute | solution.py:19
  90.5 6.0 %collective-permute-done.10 = f32[2408,16]{0,1:T(8,128)S(1)} collective-permute-done((f32[2408,16]{0,1:T(8,128)S(1)}, f32[2408,16]{0,1:T(8,128)S(1)}, u32[]{:S(2)}, u32[]{:S(2)}) %collective-permute-start.10) | collective-permute-done | bytes 154144 | tf_op jit(solution)/shard_map/ppermute | solution.py:19
  98.3 8.5 %collective-permute-done.11 = f32[2408,16]{0,1:T(8,128)S(1)} collective-permute-done((f32[2408,16]{0,1:T(8,128)S(1)}, f32[2408,16]{0,1:T(8,128)S(1)}, u32[]{:S(2)}, u32[]{:S(2)}) %collective-permute-start.11) | collective-permute-done | bytes 154144 | tf_op jit(solution)/shard_map/ppermute | solution.py:19
  106.9 6.8 %all_gather.10 = f32[2408,64]{0,1:T(8,128)S(1)} all-gather(f32[2408,16]{0,1:T(8,128)S(1)} %add.85), channel_id=1, replica_groups=mesh['lat'=8,'rad'=4] {'rad'}, dimensions={1}, use_global_device_ids=true | all-gather | bytes 770560 | tf_op jit(solution)/shard_map/all_gather | solution.py:68
  132.1 10.8 %gather_fusion.1 = f32[3072,16]{1,0:T(8,128)} fusion(f32[16,768]{0,1:T(8,128)S(1)} %copy.34, s32[3072]{0:T(1024)S(1)} %broadcast_clamp_fusion), kind=kCustom, calls=%fused_computation.1 | custom fusion | bytes 405504 | tf_op jit(solution)/shard_map/gather | solution.py:75
  144.7 3.8 %collective-permute-start.15 = (f32[1,768]{1,0:T(1,128)S(1)}, f32[1,768]{1,0:T(1,128)S(1)}, u32[]{:S(2)}, u32[]{:S(2)}) collective-permute-start(f32[1,768]{1,0:T(1,128)S(1)} %get-tuple-element.9), channel_id=1, source_target_pairs={{0,1},{1,2},{2,3},{4,5},{5,6},{6,7},{8,9},{9,10},{10,11},{12,13},{... | collective-permute-start | bytes 9224 | tf_op jit(solution)/shard_map/ppermute | solution.py:30
  149.8 3.0 %collective-permute-done.14 = f32[1,768]{1,0:T(1,128)S(1)} collective-permute-done((f32[1,768]{1,0:T(1,128)S(1)}, f32[1,768]{1,0:T(1,128)S(1)}, u32[]{:S(2)}, u32[]{:S(2)}) %collective-permute-start.14) | collective-permute-done | bytes 3104 | tf_op jit(solution)/shard_map/ppermute | solution.py:31
  152.8 3.1 %convolution_bitcast_fusion = f32[2408,16]{0,1:T(8,128)S(1)} fusion(bf16[2408,768]{1,0:T(8,128)(2,1)} %param.13, f32[16,768]{1,0:T(8,128)S(1)} %fusion.24, f32[1,768]{1,0:T(1,128)S(1)} %collective-permute-done.15, f32[1,768]{1,0:T(1,128)S(1)} %collective-permute-done.14, f32[16,768]{1,0:T(8,128)S(1)} %copy-done.2, f32[16]{0:T(128)S(1)} %copy-done.6), kind=kOutput, calls=%fused_computation.3 | convolution fusion | flops 59277312 | bytes 3957312 | tf_op jit(solution)/shard_map/dot_general | solution.py:64
  157.5 4.0 %collective-permute-done.16 = f32[2408,16]{0,1:T(8,128)S(1)} collective-permute-done((f32[2408,16]{0,1:T(8,128)S(1)}, f32[2408,16]{0,1:T(8,128)S(1)}, u32[]{:S(2)}, u32[]{:S(2)}) %collective-permute-start.16) | collective-permute-done | bytes 154144 | tf_op jit(solution)/shard_map/ppermute | solution.py:19
  161.6 6.6 %collective-permute-done.17 = f32[2408,16]{0,1:T(8,128)S(1)} collective-permute-done((f32[2408,16]{0,1:T(8,128)S(1)}, f32[2408,16]{0,1:T(8,128)S(1)}, u32[]{:S(2)}, u32[]{:S(2)}) %collective-permute-start.17) | collective-permute-done | bytes 154144 | tf_op jit(solution)/shard_map/ppermute | solution.py:19
  169.4 9.1 %collective-permute-done.18 = f32[2408,16]{0,1:T(8,128)S(1)} collective-permute-done((f32[2408,16]{0,1:T(8,128)S(1)}, f32[2408,16]{0,1:T(8,128)S(1)}, u32[]{:S(2)}, u32[]{:S(2)}) %collective-permute-start.18) | collective-permute-done | bytes 154144 | tf_op jit(solution)/shard_map/ppermute | solution.py:19
  178.6 7.4 %all_gather.11 = f32[2408,64]{0,1:T(8,128)S(1)} all-gather(f32[2408,16]{0,1:T(8,128)S(1)} %add.92), channel_id=1, replica_groups=mesh['lat'=8,'rad'=4] {'rad'}, dimensions={1}, use_global_device_ids=true | all-gather | bytes 770560 | tf_op jit(solution)/shard_map/all_gather | solution.py:68
  204.5 10.8 %gather_fusion.2 = f32[3072,16]{1,0:T(8,128)} fusion(f32[16,768]{0,1:T(8,128)S(1)} %copy.44, s32[3072]{0:T(1024)S(1)} %broadcast_clamp_fusion), kind=kCustom, calls=%fused_computation.2 | custom fusion | bytes 405504 | tf_op jit(solution)/shard_map/gather | solution.py:75
  220.4 40.0 %psum.7 = f32[3]{0:T(128)S(1)} all-reduce(f32[3]{0:T(128)S(1)} %pad_maximum_fusion.12), channel_id=1, replica_groups=mesh['lat'=8,'rad'=4] {'lat','rad'}, use_global_device_ids=true, to_apply=%region_6.0 | all-reduce | flops 3 | bytes 24 | tf_op jit(solution)/shard_map/psum | solution.py:81
  (255 shorter events, 84.5 us)
Async XLA Ops:
  0.6 41.3 %copy-start = (f32[49,64,64]{2,1,0:T(8,128)S(1)}, f32[49,64,64]{2,1,0:T(8,128)}, u32[]{:S(2)}) copy-start(f32[49,64,64]{2,1,0:T(8,128)} %param.15) | copy-start | bytes 2408452
  1.5 3.7 %collective-permute-start.1 = (f32[1,768]{1,0:T(1,128)S(1)}, f32[1,768]{1,0:T(1,128)S(1)}, u32[]{:S(2)}, u32[]{:S(2)}) collective-permute-start(f32[1,768]{1,0:T(1,128)S(1)} %get-tuple-element.17), channel_id=1, source_target_pairs={{0,1},{1,2},{2,3},{4,5},{5,6},{6,7},{8,9},{9,10},{10,11},{12,13},{... | collective-permute-start | bytes 9224 | tf_op jit(solution)/shard_map/ppermute | solution.py:30
  3.9 23.4 %copy-start.5 = (s32[4,768]{1,0:T(4,128)S(1)}, s32[4,768]{1,0:T(4,128)}, u32[]{:S(2)}) copy-start(s32[4,768]{1,0:T(4,128)} %param.14) | copy-start | bytes 36868
  3.9 5.2 %collective-permute-start = (f32[1,768]{1,0:T(1,128)S(1)}, f32[1,768]{1,0:T(1,128)S(1)}, u32[]{:S(2)}, u32[]{:S(2)}) collective-permute-start(f32[1,768]{1,0:T(1,128)S(1)} %get-tuple-element.16), channel_id=1, source_target_pairs={{1,0},{2,1},{3,2},{5,4},{6,5},{7,6},{9,8},{10,9},{11,10},{13,12},{... | collective-permute-start | bytes 9224 | tf_op jit(solution)/shard_map/ppermute | solution.py:31
  12.3 5.5 %collective-permute-start.2 = (f32[2408,16]{0,1:T(8,128)S(1)}, f32[2408,16]{0,1:T(8,128)S(1)}, u32[]{:S(2)}, u32[]{:S(2)}) collective-permute-start(f32[2408,16]{0,1:T(8,128)S(1)} %convolution_bitcast_fusion.2), channel_id=1, source_target_pairs={{0,4},{4,0},{8,12},{12,8},{16,20},{20,16},{24,28},{28,24},{1,5},{5... | collective-permute-start | bytes 462344 | tf_op jit(solution)/shard_map/ppermute | solution.py:19
  17.9 6.7 %collective-permute-start.3 = (f32[2408,16]{0,1:T(8,128)S(1)}, f32[2408,16]{0,1:T(8,128)S(1)}, u32[]{:S(2)}, u32[]{:S(2)}) collective-permute-start(f32[2408,16]{0,1:T(8,128)S(1)} %add.74), channel_id=1, source_target_pairs={{0,8},{4,12},{8,0},{12,4},{16,24},{20,28},{24,16},{28,20},{1,9},{5... | collective-permute-start | bytes 462344 | tf_op jit(solution)/shard_map/ppermute | solution.py:19
  24.6 10.3 %collective-permute-start.4 = (f32[2408,16]{0,1:T(8,128)S(1)}, f32[2408,16]{0,1:T(8,128)S(1)}, u32[]{:S(2)}, u32[]{:S(2)}) collective-permute-start(f32[2408,16]{0,1:T(8,128)S(1)} %add.75), channel_id=1, source_target_pairs={{0,16},{4,20},{8,24},{12,28},{16,0},{20,4},{24,8},{28,12},{1,17},{... | collective-permute-start | bytes 462344 | tf_op jit(solution)/shard_map/ppermute | solution.py:19
  56.6 16.3 %collective-permute-start.6 = (f32[1,768]{1,0:T(1,128)S(1)}, f32[1,768]{1,0:T(1,128)S(1)}, u32[]{:S(2)}, u32[]{:S(2)}) collective-permute-start(f32[1,768]{1,0:T(1,128)S(1)} %get-tuple-element.15), channel_id=1, source_target_pairs={{0,1},{1,2},{2,3},{4,5},{5,6},{6,7},{8,9},{9,10},{10,11},{12,13},{... | collective-permute-start | bytes 9224 | tf_op jit(solution)/shard_map/ppermute | solution.py:30
  58.8 14.1 %collective-permute-start.5 = (f32[1,768]{1,0:T(1,128)S(1)}, f32[1,768]{1,0:T(1,128)S(1)}, u32[]{:S(2)}, u32[]{:S(2)}) collective-permute-start(f32[1,768]{1,0:T(1,128)S(1)} %get-tuple-element.14), channel_id=1, source_target_pairs={{1,0},{2,1},{3,2},{5,4},{6,5},{7,6},{9,8},{10,9},{11,10},{13,12},{... | collective-permute-start | bytes 9224 | tf_op jit(solution)/shard_map/ppermute | solution.py:31
  71.2 9.9 %copy-start.6 = (f32[16]{0:T(128)S(1)}, f32[16]{0:T(128)}, u32[]{:S(2)}) copy-start(f32[16]{0:T(128)} %param.11) | copy-start | bytes 196
  73.0 5.1 %collective-permute-start.8 = (f32[1,768]{1,0:T(1,128)S(1)}, f32[1,768]{1,0:T(1,128)S(1)}, u32[]{:S(2)}, u32[]{:S(2)}) collective-permute-start(f32[1,768]{1,0:T(1,128)S(1)} %get-tuple-element.13), channel_id=1, source_target_pairs={{0,1},{1,2},{2,3},{4,5},{5,6},{6,7},{8,9},{9,10},{10,11},{12,13},{... | collective-permute-start | bytes 9224 | tf_op jit(solution)/shard_map/ppermute | solution.py:30
  76.8 4.3 %collective-permute-start.7 = (f32[1,768]{1,0:T(1,128)S(1)}, f32[1,768]{1,0:T(1,128)S(1)}, u32[]{:S(2)}, u32[]{:S(2)}) collective-permute-start(f32[1,768]{1,0:T(1,128)S(1)} %get-tuple-element.12), channel_id=1, source_target_pairs={{1,0},{2,1},{3,2},{5,4},{6,5},{7,6},{9,8},{10,9},{11,10},{13,12},{... | collective-permute-start | bytes 9224 | tf_op jit(solution)/shard_map/ppermute | solution.py:31
  84.2 5.5 %collective-permute-start.9 = (f32[2408,16]{0,1:T(8,128)S(1)}, f32[2408,16]{0,1:T(8,128)S(1)}, u32[]{:S(2)}, u32[]{:S(2)}) collective-permute-start(f32[2408,16]{0,1:T(8,128)S(1)} %convolution_bitcast_fusion.1), channel_id=1, source_target_pairs={{0,4},{4,0},{8,12},{12,8},{16,20},{20,16},{24,28},{28,24},{1,5},{5... | collective-permute-start | bytes 462344 | tf_op jit(solution)/shard_map/ppermute | solution.py:19
  89.8 6.7 %collective-permute-start.10 = (f32[2408,16]{0,1:T(8,128)S(1)}, f32[2408,16]{0,1:T(8,128)S(1)}, u32[]{:S(2)}, u32[]{:S(2)}) collective-permute-start(f32[2408,16]{0,1:T(8,128)S(1)} %add.83), channel_id=1, source_target_pairs={{0,8},{4,12},{8,0},{12,4},{16,24},{20,28},{24,16},{28,20},{1,9},{5... | collective-permute-start | bytes 462344 | tf_op jit(solution)/shard_map/ppermute | solution.py:19
  96.5 10.3 %collective-permute-start.11 = (f32[2408,16]{0,1:T(8,128)S(1)}, f32[2408,16]{0,1:T(8,128)S(1)}, u32[]{:S(2)}, u32[]{:S(2)}) collective-permute-start(f32[2408,16]{0,1:T(8,128)S(1)} %add.84), channel_id=1, source_target_pairs={{0,16},{4,20},{8,24},{12,28},{16,0},{20,4},{24,8},{28,12},{1,17},{... | collective-permute-start | bytes 462344 | tf_op jit(solution)/shard_map/ppermute | solution.py:19
  128.4 16.3 %collective-permute-start.13 = (f32[1,768]{1,0:T(1,128)S(1)}, f32[1,768]{1,0:T(1,128)S(1)}, u32[]{:S(2)}, u32[]{:S(2)}) collective-permute-start(f32[1,768]{1,0:T(1,128)S(1)} %get-tuple-element.11), channel_id=1, source_target_pairs={{0,1},{1,2},{2,3},{4,5},{5,6},{6,7},{8,9},{9,10},{10,11},{12,13},{... | collective-permute-start | bytes 9224 | tf_op jit(solution)/shard_map/ppermute | solution.py:30
  130.7 14.0 %collective-permute-start.12 = (f32[1,768]{1,0:T(1,128)S(1)}, f32[1,768]{1,0:T(1,128)S(1)}, u32[]{:S(2)}, u32[]{:S(2)}) collective-permute-start(f32[1,768]{1,0:T(1,128)S(1)} %get-tuple-element.10), channel_id=1, source_target_pairs={{1,0},{2,1},{3,2},{5,4},{6,5},{7,6},{9,8},{10,9},{11,10},{13,12},{... | collective-permute-start | bytes 9224 | tf_op jit(solution)/shard_map/ppermute | solution.py:31
  144.7 5.1 %collective-permute-start.15 = (f32[1,768]{1,0:T(1,128)S(1)}, f32[1,768]{1,0:T(1,128)S(1)}, u32[]{:S(2)}, u32[]{:S(2)}) collective-permute-start(f32[1,768]{1,0:T(1,128)S(1)} %get-tuple-element.9), channel_id=1, source_target_pairs={{0,1},{1,2},{2,3},{4,5},{5,6},{6,7},{8,9},{9,10},{10,11},{12,13},{... | collective-permute-start | bytes 9224 | tf_op jit(solution)/shard_map/ppermute | solution.py:30
  148.5 4.3 %collective-permute-start.14 = (f32[1,768]{1,0:T(1,128)S(1)}, f32[1,768]{1,0:T(1,128)S(1)}, u32[]{:S(2)}, u32[]{:S(2)}) collective-permute-start(f32[1,768]{1,0:T(1,128)S(1)} %get-tuple-element.8), channel_id=1, source_target_pairs={{1,0},{2,1},{3,2},{5,4},{6,5},{7,6},{9,8},{10,9},{11,10},{13,12},{... | collective-permute-start | bytes 9224 | tf_op jit(solution)/shard_map/ppermute | solution.py:31
  155.9 5.5 %collective-permute-start.16 = (f32[2408,16]{0,1:T(8,128)S(1)}, f32[2408,16]{0,1:T(8,128)S(1)}, u32[]{:S(2)}, u32[]{:S(2)}) collective-permute-start(f32[2408,16]{0,1:T(8,128)S(1)} %convolution_bitcast_fusion), channel_id=1, source_target_pairs={{0,4},{4,0},{8,12},{12,8},{16,20},{20,16},{24,28},{28,24},{1,5},{5... | collective-permute-start | bytes 462344 | tf_op jit(solution)/shard_map/ppermute | solution.py:19
  161.5 6.7 %collective-permute-start.17 = (f32[2408,16]{0,1:T(8,128)S(1)}, f32[2408,16]{0,1:T(8,128)S(1)}, u32[]{:S(2)}, u32[]{:S(2)}) collective-permute-start(f32[2408,16]{0,1:T(8,128)S(1)} %add.90), channel_id=1, source_target_pairs={{0,8},{4,12},{8,0},{12,4},{16,24},{20,28},{24,16},{28,20},{1,9},{5... | collective-permute-start | bytes 462344 | tf_op jit(solution)/shard_map/ppermute | solution.py:19
  168.2 10.3 %collective-permute-start.18 = (f32[2408,16]{0,1:T(8,128)S(1)}, f32[2408,16]{0,1:T(8,128)S(1)}, u32[]{:S(2)}, u32[]{:S(2)}) collective-permute-start(f32[2408,16]{0,1:T(8,128)S(1)} %add.91), channel_id=1, source_target_pairs={{0,16},{4,20},{8,24},{12,28},{16,0},{20,4},{24,8},{28,12},{1,17},{... | collective-permute-start | bytes 462344 | tf_op jit(solution)/shard_map/ppermute | solution.py:19
  200.8 16.3 %collective-permute-start.20 = (f32[1,768]{1,0:T(1,128)S(1)}, f32[1,768]{1,0:T(1,128)S(1)}, u32[]{:S(2)}, u32[]{:S(2)}) collective-permute-start(f32[1,768]{1,0:T(1,128)S(1)} %get-tuple-element.7), channel_id=1, source_target_pairs={{0,1},{1,2},{2,3},{4,5},{5,6},{6,7},{8,9},{9,10},{10,11},{12,13},{... | collective-permute-start | bytes 9224 | tf_op jit(solution)/shard_map/ppermute | solution.py:30
  203.0 14.0 %collective-permute-start.19 = (f32[1,768]{1,0:T(1,128)S(1)}, f32[1,768]{1,0:T(1,128)S(1)}, u32[]{:S(2)}, u32[]{:S(2)}) collective-permute-start(f32[1,768]{1,0:T(1,128)S(1)} %get-tuple-element.6), channel_id=1, source_target_pairs={{1,0},{2,1},{3,2},{5,4},{6,5},{7,6},{9,8},{10,9},{11,10},{13,12},{... | collective-permute-start | bytes 9224 | tf_op jit(solution)/shard_map/ppermute | solution.py:31
  (4 other events, 19.7 us)
